TPU v7x, 32 devices: a whole 2x2x4 slice. The times are simulated.
32 devices in a mesh: row: 4 (over z), col: 8 (over y, x, core).
Axes of the slice: x: 2, y: 2, z: 4, core: 2. Of those that a mesh axis runs over, the one named last changes fastest.
Arguments:
- adjacency: int32 [32768, 2048], P('col', 'row'), may hold values from -2147483648 to 2147483647, as said below
- frontier: bfloat16 [65536, 128], P(('row', 'col')), may hold values from 0 to 1, as said below
- visited: int32 [4, 32768], P(None, ('col', 'row')), may hold values from -2147483648 to 2147483647, as said below
Outputs:
- path_counts: float32 [32768, 128], P(('col', 'row'))
- reached_bits: int32 [4, 32768], P(None, ('col', 'row'))
Inputs may be any that keep to these rules, and one draw needn't show every extreme that they name: Bit k of adjacency[d, w] is the edge from source vertex 32 w + k to destination d; degrees and edge densities differ between vertices and between blocks of 128 by 128 vertices. `frontier`: values are zero or between 0.1 and 1. Bit k of visited[w, d] tells whether destination d was reached from root 32 w + k.
All inputs are finite; a program needn't handle non-finite values.
Results may differ from a plain program's by a relative error of at most 0.0003.
Values may be sent and summed in bfloat16 or wider, within the bound.
A program may use at most 64 MiB of HBM per device.

v0:
```python
import functools
import math
import jax
import jax.numpy as jnp
from jax import lax
from jax.sharding import PartitionSpec as P


def expand_bits(packed):
    shift_table = jnp.arange(32, dtype=jnp.int32)
    bit_table = jnp.bitwise_and(jnp.right_shift(packed[:, :, None], shift_table), 1)
    return bit_table.reshape(packed.shape[0], packed.shape[1] * 32).astype(jnp.bfloat16)


def tile_product(packed, vectors):
    row_total = packed.shape[0]
    src_width = vectors.shape[0]
    row_len = math.gcd(row_total, 1024)
    block_len = math.gcd(src_width, 4096)
    block_count = src_width // block_len
    row_blocks = packed.reshape(row_total // row_len, row_len, packed.shape[1])

    def one_rows(packed_rows):
        initial = jnp.zeros((row_len, vectors.shape[1]), jnp.float32)

        def add_block(turn_index, total):
            offset = turn_index * block_len
            packed_cols = lax.dynamic_slice_in_dim(packed_rows, offset // 32, block_len // 32, 1)
            vector_rows = lax.dynamic_slice_in_dim(vectors, offset, block_len, 0)
            return total + jnp.dot(
                expand_bits(packed_cols), vector_rows, preferred_element_type=jnp.float32
            )

        return lax.fori_loop(0, block_count, add_block, initial)

    return lax.map(one_rows, row_blocks).reshape(row_total, vectors.shape[1])


def finish(reached, visited):
    row_count = reached.shape[0]
    word_count = visited.shape[0]
    shift_table = jnp.arange(32, dtype=jnp.int32)
    seen_bits = jnp.bitwise_and(jnp.right_shift(visited[:, :, None], shift_table), 1)
    seen_bits = jnp.transpose(seen_bits, (1, 0, 2)).reshape(row_count, word_count * 32)
    path_counts = jnp.where(seen_bits == 1, jnp.float32(0.0), reached)
    fresh = jnp.logical_and(seen_bits == 0, reached > 0).astype(jnp.int32)
    fresh = fresh.reshape(row_count, word_count, 32)
    added = functools.reduce(
        jnp.bitwise_or, [jnp.left_shift(fresh[:, :, position], position) for position in range(32)]
    )
    reached_bits = jnp.bitwise_or(visited, jnp.transpose(added))
    return (path_counts, reached_bits)


def shards(adjacency, frontier, visited):
    partial_sum = tile_product(adjacency, lax.all_gather(frontier, "col", axis=0, tiled=True))
    reached = lax.psum_scatter(partial_sum, "row", scatter_dimension=0, tiled=True)
    return finish(reached, visited)


def solution(mesh):
    placed = (P("col", "row"), P(("row", "col"), None), P(None, ("col", "row")))
    return jax.shard_map(
        shards,
        mesh=mesh,
        in_specs=placed,
        out_specs=(P(("col", "row"), None), P(None, ("col", "row"))),
        check_vma=False,
    )
```

profile of v0, /device:TPU:0, one launch (start us, length us, event | category | flops | bytes accessed | tf_op | source)
XLA Modules:
  0.0 302.6 jit_solution(3641786768029354774)
XLA Ops:
  8.0 41.2 %all-gather.2.cloned.1.call-done = bf16[16384,128]{1,0:T(8,128)(2,1)} async-done(((bf16[2048,128]{1,0:T(8,128)(2,1)}), bf16[16384,128]{1,0:T(8,128)(2,1)}) %all-gather.2.cloned.1.call-update) | async-done | bytes 4194320 | tf_op jit(solution)/shard_map/all_gather | solution.py:56
  49.2 195.2 %while.36 = (s32[]{:T(128)}, f32[4,1024,128]{2,1,0:T(8,128)}, s32[4,1024,512]{2,1,0:T(8,128)}, bf16[16384,128]{1,0:T(8,128)(2,1)}, s32[]{:T(128)}, /*index=5*/s3...) while((s32[]{:T(128)}, f32[4,1024,128]{2,1,0:T(8,128)}, ...), condition=%wide.region_3.4_spmd, body=%wide.region_0.3_spmd.sunk | while | flops 1086586880 | bytes 29951060 | solution.py:36
  54.2 42.9 %while.37 = (s32[]{:T(128)}, f32[1024,128]{1,0:T(8,128)S(1)}, s32[1024,512]{0,1:T(8,128)S(1)}, bf16[16384,128]{1,0:T(8,128)(2,1)}, s32[]{:T(128)}, /*index=5*/s3...) while((s32[]{:T(128)}, f32[1024,128]{1,0:T(8,128)S(1)}, ...), condition=%wide.region_2.2_spmd.clone, body=%wide.region_1.1_spmd.clone.sunk | while | flops 1086586880 | bytes 20513124 | solution.py:34
  54.4 4.4 %fusion.66 = bf16[1024,4096]{0,1:T(8,128)(2,1)} fusion(s32[4096]{0:T(1024)S(1)} %shift_right_arithmetic.108, s32[1024,128]{0,1:T(8,128)S(1)} %constant_dynamic-slice_fusion.5), kind=kLoop, calls=%fused_computation.2.clone.1 | loop fusion | flops 12582912 | bytes 8929280 | tf_op jit(solution)/shard_map/while/body/eval_jaxpr/while/body/eval_jaxpr/convert_element_type | solution.py:12
  58.9 6.1 %convolution_add_fusion.2 = f32[1024,128]{1,0:T(8,128)S(1)} fusion(bf16[1024,4096]{0,1:T(8,128)(2,1)} %fusion.66, bf16[16384,128]{1,0:T(8,128)(2,1)} %get-tuple-element.340, s32[]{:T(128)S(6)} %select_n.46, f32[1024,128]{1,0:T(8,128)S(1)} %get-tuple-element.326, pred[]{:T(512)S(6)} %compare.13), kind=kOutput, calls=%fused_computation.3.clone.1 | convolution fusion | flops 1074003968 | bytes 10485765 | tf_op jit(solution)/shard_map/while/body/eval_jaxpr/while/body/eval_jaxpr/dot_general | solution.py:30
  65.2 4.4 %fusion.66 = bf16[1024,4096]{0,1:T(8,128)(2,1)} fusion(s32[4096]{0:T(1024)S(1)} %shift_right_arithmetic.108, s32[1024,128]{0,1:T(8,128)S(1)} %constant_dynamic-slice_fusion.5), kind=kLoop, calls=%fused_computation.2.clone.1 | loop fusion | flops 12582912 | bytes 8929280 | tf_op jit(solution)/shard_map/while/body/eval_jaxpr/while/body/eval_jaxpr/convert_element_type | solution.py:12
  69.6 6.1 %convolution_add_fusion.2 = f32[1024,128]{1,0:T(8,128)S(1)} fusion(bf16[1024,4096]{0,1:T(8,128)(2,1)} %fusion.66, bf16[16384,128]{1,0:T(8,128)(2,1)} %get-tuple-element.340, s32[]{:T(128)S(6)} %select_n.46, f32[1024,128]{1,0:T(8,128)S(1)} %get-tuple-element.326, pred[]{:T(512)S(6)} %compare.13), kind=kOutput, calls=%fused_computation.3.clone.1 | convolution fusion | flops 1074003968 | bytes 10485765 | tf_op jit(solution)/shard_map/while/body/eval_jaxpr/while/body/eval_jaxpr/dot_general | solution.py:30
  75.9 4.4 %fusion.66 = bf16[1024,4096]{0,1:T(8,128)(2,1)} fusion(s32[4096]{0:T(1024)S(1)} %shift_right_arithmetic.108, s32[1024,128]{0,1:T(8,128)S(1)} %constant_dynamic-slice_fusion.5), kind=kLoop, calls=%fused_computation.2.clone.1 | loop fusion | flops 12582912 | bytes 8929280 | tf_op jit(solution)/shard_map/while/body/eval_jaxpr/while/body/eval_jaxpr/convert_element_type | solution.py:12
  80.3 6.1 %convolution_add_fusion.2 = f32[1024,128]{1,0:T(8,128)S(1)} fusion(bf16[1024,4096]{0,1:T(8,128)(2,1)} %fusion.66, bf16[16384,128]{1,0:T(8,128)(2,1)} %get-tuple-element.340, s32[]{:T(128)S(6)} %select_n.46, f32[1024,128]{1,0:T(8,128)S(1)} %get-tuple-element.326, pred[]{:T(512)S(6)} %compare.13), kind=kOutput, calls=%fused_computation.3.clone.1 | convolution fusion | flops 1074003968 | bytes 10485765 | tf_op jit(solution)/shard_map/while/body/eval_jaxpr/while/body/eval_jaxpr/dot_general | solution.py:30
  86.6 4.4 %fusion.66 = bf16[1024,4096]{0,1:T(8,128)(2,1)} fusion(s32[4096]{0:T(1024)S(1)} %shift_right_arithmetic.108, s32[1024,128]{0,1:T(8,128)S(1)} %constant_dynamic-slice_fusion.5), kind=kLoop, calls=%fused_computation.2.clone.1 | loop fusion | flops 12582912 | bytes 8929280 | tf_op jit(solution)/shard_map/while/body/eval_jaxpr/while/body/eval_jaxpr/convert_element_type | solution.py:12
  91.1 6.1 %convolution_add_fusion.2 = f32[1024,128]{1,0:T(8,128)S(1)} fusion(bf16[1024,4096]{0,1:T(8,128)(2,1)} %fusion.66, bf16[16384,128]{1,0:T(8,128)(2,1)} %get-tuple-element.340, s32[]{:T(128)S(6)} %select_n.46, f32[1024,128]{1,0:T(8,128)S(1)} %get-tuple-element.326, pred[]{:T(512)S(6)} %compare.13), kind=kOutput, calls=%fused_computation.3.clone.1 | convolution fusion | flops 1074003968 | bytes 10485765 | tf_op jit(solution)/shard_map/while/body/eval_jaxpr/while/body/eval_jaxpr/dot_general | solution.py:30
  103.1 42.9 %while.37 = (s32[]{:T(128)}, f32[1024,128]{1,0:T(8,128)S(1)}, s32[1024,512]{0,1:T(8,128)S(1)}, bf16[16384,128]{1,0:T(8,128)(2,1)}, s32[]{:T(128)}, /*index=5*/s3...) while((s32[]{:T(128)}, f32[1024,128]{1,0:T(8,128)S(1)}, ...), condition=%wide.region_2.2_spmd.clone, body=%wide.region_1.1_spmd.clone.sunk | while | flops 1086586880 | bytes 20513124 | solution.py:34
  103.3 4.4 %fusion.66 = bf16[1024,4096]{0,1:T(8,128)(2,1)} fusion(s32[4096]{0:T(1024)S(1)} %shift_right_arithmetic.108, s32[1024,128]{0,1:T(8,128)S(1)} %constant_dynamic-slice_fusion.5), kind=kLoop, calls=%fused_computation.2.clone.1 | loop fusion | flops 12582912 | bytes 8929280 | tf_op jit(solution)/shard_map/while/body/eval_jaxpr/while/body/eval_jaxpr/convert_element_type | solution.py:12
  107.7 6.1 %convolution_add_fusion.2 = f32[1024,128]{1,0:T(8,128)S(1)} fusion(bf16[1024,4096]{0,1:T(8,128)(2,1)} %fusion.66, bf16[16384,128]{1,0:T(8,128)(2,1)} %get-tuple-element.340, s32[]{:T(128)S(6)} %select_n.46, f32[1024,128]{1,0:T(8,128)S(1)} %get-tuple-element.326, pred[]{:T(512)S(6)} %compare.13), kind=kOutput, calls=%fused_computation.3.clone.1 | convolution fusion | flops 1074003968 | bytes 10485765 | tf_op jit(solution)/shard_map/while/body/eval_jaxpr/while/body/eval_jaxpr/dot_general | solution.py:30
  114.0 4.4 %fusion.66 = bf16[1024,4096]{0,1:T(8,128)(2,1)} fusion(s32[4096]{0:T(1024)S(1)} %shift_right_arithmetic.108, s32[1024,128]{0,1:T(8,128)S(1)} %constant_dynamic-slice_fusion.5), kind=kLoop, calls=%fused_computation.2.clone.1 | loop fusion | flops 12582912 | bytes 8929280 | tf_op jit(solution)/shard_map/while/body/eval_jaxpr/while/body/eval_jaxpr/convert_element_type | solution.py:12
  118.4 6.1 %convolution_add_fusion.2 = f32[1024,128]{1,0:T(8,128)S(1)} fusion(bf16[1024,4096]{0,1:T(8,128)(2,1)} %fusion.66, bf16[16384,128]{1,0:T(8,128)(2,1)} %get-tuple-element.340, s32[]{:T(128)S(6)} %select_n.46, f32[1024,128]{1,0:T(8,128)S(1)} %get-tuple-element.326, pred[]{:T(512)S(6)} %compare.13), kind=kOutput, calls=%fused_computation.3.clone.1 | convolution fusion | flops 1074003968 | bytes 10485765 | tf_op jit(solution)/shard_map/while/body/eval_jaxpr/while/body/eval_jaxpr/dot_general | solution.py:30
  124.7 4.4 %fusion.66 = bf16[1024,4096]{0,1:T(8,128)(2,1)} fusion(s32[4096]{0:T(1024)S(1)} %shift_right_arithmetic.108, s32[1024,128]{0,1:T(8,128)S(1)} %constant_dynamic-slice_fusion.5), kind=kLoop, calls=%fused_computation.2.clone.1 | loop fusion | flops 12582912 | bytes 8929280 | tf_op jit(solution)/shard_map/while/body/eval_jaxpr/while/body/eval_jaxpr/convert_element_type | solution.py:12
  129.2 6.1 %convolution_add_fusion.2 = f32[1024,128]{1,0:T(8,128)S(1)} fusion(bf16[1024,4096]{0,1:T(8,128)(2,1)} %fusion.66, bf16[16384,128]{1,0:T(8,128)(2,1)} %get-tuple-element.340, s32[]{:T(128)S(6)} %select_n.46, f32[1024,128]{1,0:T(8,128)S(1)} %get-tuple-element.326, pred[]{:T(512)S(6)} %compare.13), kind=kOutput, calls=%fused_computation.3.clone.1 | convolution fusion | flops 1074003968 | bytes 10485765 | tf_op jit(solution)/shard_map/while/body/eval_jaxpr/while/body/eval_jaxpr/dot_general | solution.py:30
  135.5 4.4 %fusion.66 = bf16[1024,4096]{0,1:T(8,128)(2,1)} fusion(s32[4096]{0:T(1024)S(1)} %shift_right_arithmetic.108, s32[1024,128]{0,1:T(8,128)S(1)} %constant_dynamic-slice_fusion.5), kind=kLoop, calls=%fused_computation.2.clone.1 | loop fusion | flops 12582912 | bytes 8929280 | tf_op jit(solution)/shard_map/while/body/eval_jaxpr/while/body/eval_jaxpr/convert_element_type | solution.py:12
  139.9 6.1 %convolution_add_fusion.2 = f32[1024,128]{1,0:T(8,128)S(1)} fusion(bf16[1024,4096]{0,1:T(8,128)(2,1)} %fusion.66, bf16[16384,128]{1,0:T(8,128)(2,1)} %get-tuple-element.340, s32[]{:T(128)S(6)} %select_n.46, f32[1024,128]{1,0:T(8,128)S(1)} %get-tuple-element.326, pred[]{:T(512)S(6)} %compare.13), kind=kOutput, calls=%fused_computation.3.clone.1 | convolution fusion | flops 1074003968 | bytes 10485765 | tf_op jit(solution)/shard_map/while/body/eval_jaxpr/while/body/eval_jaxpr/dot_general | solution.py:30
  151.9 42.9 %while.37 = (s32[]{:T(128)}, f32[1024,128]{1,0:T(8,128)S(1)}, s32[1024,512]{0,1:T(8,128)S(1)}, bf16[16384,128]{1,0:T(8,128)(2,1)}, s32[]{:T(128)}, /*index=5*/s3...) while((s32[]{:T(128)}, f32[1024,128]{1,0:T(8,128)S(1)}, ...), condition=%wide.region_2.2_spmd.clone, body=%wide.region_1.1_spmd.clone.sunk | while | flops 1086586880 | bytes 20513124 | solution.py:34
  152.1 4.4 %fusion.66 = bf16[1024,4096]{0,1:T(8,128)(2,1)} fusion(s32[4096]{0:T(1024)S(1)} %shift_right_arithmetic.108, s32[1024,128]{0,1:T(8,128)S(1)} %constant_dynamic-slice_fusion.5), kind=kLoop, calls=%fused_computation.2.clone.1 | loop fusion | flops 12582912 | bytes 8929280 | tf_op jit(solution)/shard_map/while/body/eval_jaxpr/while/body/eval_jaxpr/convert_element_type | solution.py:12
  156.5 6.1 %convolution_add_fusion.2 = f32[1024,128]{1,0:T(8,128)S(1)} fusion(bf16[1024,4096]{0,1:T(8,128)(2,1)} %fusion.66, bf16[16384,128]{1,0:T(8,128)(2,1)} %get-tuple-element.340, s32[]{:T(128)S(6)} %select_n.46, f32[1024,128]{1,0:T(8,128)S(1)} %get-tuple-element.326, pred[]{:T(512)S(6)} %compare.13), kind=kOutput, calls=%fused_computation.3.clone.1 | convolution fusion | flops 1074003968 | bytes 10485765 | tf_op jit(solution)/shard_map/while/body/eval_jaxpr/while/body/eval_jaxpr/dot_general | solution.py:30
  167.2 6.1 %convolution_add_fusion.2 = f32[1024,128]{1,0:T(8,128)S(1)} fusion(bf16[1024,4096]{0,1:T(8,128)(2,1)} %fusion.66, bf16[16384,128]{1,0:T(8,128)(2,1)} %get-tuple-element.340, s32[]{:T(128)S(6)} %select_n.46, f32[1024,128]{1,0:T(8,128)S(1)} %get-tuple-element.326, pred[]{:T(512)S(6)} %compare.13), kind=kOutput, calls=%fused_computation.3.clone.1 | convolution fusion | flops 1074003968 | bytes 10485765 | tf_op jit(solution)/shard_map/while/body/eval_jaxpr/while/body/eval_jaxpr/dot_general | solution.py:30
  178.0 6.1 %convolution_add_fusion.2 = f32[1024,128]{1,0:T(8,128)S(1)} fusion(bf16[1024,4096]{0,1:T(8,128)(2,1)} %fusion.66, bf16[16384,128]{1,0:T(8,128)(2,1)} %get-tuple-element.340, s32[]{:T(128)S(6)} %select_n.46, f32[1024,128]{1,0:T(8,128)S(1)} %get-tuple-element.326, pred[]{:T(512)S(6)} %compare.13), kind=kOutput, calls=%fused_computation.3.clone.1 | convolution fusion | flops 1074003968 | bytes 10485765 | tf_op jit(solution)/shard_map/while/body/eval_jaxpr/while/body/eval_jaxpr/dot_general | solution.py:30
  188.7 6.1 %convolution_add_fusion.2 = f32[1024,128]{1,0:T(8,128)S(1)} fusion(bf16[1024,4096]{0,1:T(8,128)(2,1)} %fusion.66, bf16[16384,128]{1,0:T(8,128)(2,1)} %get-tuple-element.340, s32[]{:T(128)S(6)} %select_n.46, f32[1024,128]{1,0:T(8,128)S(1)} %get-tuple-element.326, pred[]{:T(512)S(6)} %compare.13), kind=kOutput, calls=%fused_computation.3.clone.1 | convolution fusion | flops 1074003968 | bytes 10485765 | tf_op jit(solution)/shard_map/while/body/eval_jaxpr/while/body/eval_jaxpr/dot_general | solution.py:30
  200.7 42.9 %while.37 = (s32[]{:T(128)}, f32[1024,128]{1,0:T(8,128)S(1)}, s32[1024,512]{0,1:T(8,128)S(1)}, bf16[16384,128]{1,0:T(8,128)(2,1)}, s32[]{:T(128)}, /*index=5*/s3...) while((s32[]{:T(128)}, f32[1024,128]{1,0:T(8,128)S(1)}, ...), condition=%wide.region_2.2_spmd.clone, body=%wide.region_1.1_spmd.clone.sunk | while | flops 1086586880 | bytes 20513124 | solution.py:34
  205.3 6.1 %convolution_add_fusion.2 = f32[1024,128]{1,0:T(8,128)S(1)} fusion(bf16[1024,4096]{0,1:T(8,128)(2,1)} %fusion.66, bf16[16384,128]{1,0:T(8,128)(2,1)} %get-tuple-element.340, s32[]{:T(128)S(6)} %select_n.46, f32[1024,128]{1,0:T(8,128)S(1)} %get-tuple-element.326, pred[]{:T(512)S(6)} %compare.13), kind=kOutput, calls=%fused_computation.3.clone.1 | convolution fusion | flops 1074003968 | bytes 10485765 | tf_op jit(solution)/shard_map/while/body/eval_jaxpr/while/body/eval_jaxpr/dot_general | solution.py:30
  216.1 6.1 %convolution_add_fusion.2 = f32[1024,128]{1,0:T(8,128)S(1)} fusion(bf16[1024,4096]{0,1:T(8,128)(2,1)} %fusion.66, bf16[16384,128]{1,0:T(8,128)(2,1)} %get-tuple-element.340, s32[]{:T(128)S(6)} %select_n.46, f32[1024,128]{1,0:T(8,128)S(1)} %get-tuple-element.326, pred[]{:T(512)S(6)} %compare.13), kind=kOutput, calls=%fused_computation.3.clone.1 | convolution fusion | flops 1074003968 | bytes 10485765 | tf_op jit(solution)/shard_map/while/body/eval_jaxpr/while/body/eval_jaxpr/dot_general | solution.py:30
  226.8 6.1 %convolution_add_fusion.2 = f32[1024,128]{1,0:T(8,128)S(1)} fusion(bf16[1024,4096]{0,1:T(8,128)(2,1)} %fusion.66, bf16[16384,128]{1,0:T(8,128)(2,1)} %get-tuple-element.340, s32[]{:T(128)S(6)} %select_n.46, f32[1024,128]{1,0:T(8,128)S(1)} %get-tuple-element.326, pred[]{:T(512)S(6)} %compare.13), kind=kOutput, calls=%fused_computation.3.clone.1 | convolution fusion | flops 1074003968 | bytes 10485765 | tf_op jit(solution)/shard_map/while/body/eval_jaxpr/while/body/eval_jaxpr/dot_general | solution.py:30
  237.5 6.1 %convolution_add_fusion.2 = f32[1024,128]{1,0:T(8,128)S(1)} fusion(bf16[1024,4096]{0,1:T(8,128)(2,1)} %fusion.66, bf16[16384,128]{1,0:T(8,128)(2,1)} %get-tuple-element.340, s32[]{:T(128)S(6)} %select_n.46, f32[1024,128]{1,0:T(8,128)S(1)} %get-tuple-element.326, pred[]{:T(512)S(6)} %compare.13), kind=kOutput, calls=%fused_computation.3.clone.1 | convolution fusion | flops 1074003968 | bytes 10485765 | tf_op jit(solution)/shard_map/while/body/eval_jaxpr/while/body/eval_jaxpr/dot_general | solution.py:30
  247.5 43.7 %reduce-scatter.2.cloned.1.call-done = f32[1024,128]{0,1:T(8,128)} async-done(((f32[4096,128]{0,1:T(8,128)}), f32[1024,128]{0,1:T(8,128)}) %reduce-scatter.2.cloned.1.call-update) | async-done | bytes 524304 | tf_op jit(solution)/shard_map/reduce_scatter | solution.py:57
  (87 shorter events, 65.1 us)
Async XLA Ops:
  7.2 42.0 %all-gather.2.cloned.1.call-start = ((), (), s32[]{:S(2)}) async-start(), calls=%async_computation.1 | async-start | bytes 4718592 | tf_op jit(solution)/shard_map/all_gather | solution.py:56
  7.9 283.3 %reduce-scatter.2.cloned.1.call-start = ((), (), s32[]{:S(2)}) async-start(), calls=%async_computation.2 | async-start | bytes 2621440 | tf_op jit(solution)/shard_map/reduce_scatter | solution.py:57
  244.4 46.7 %copy-start = (s32[4,1024]{1,0:T(4,128)S(1)}, s32[4,1024]{1,0:T(4,128)}, u32[]{:S(2)}) copy-start(s32[4,1024]{1,0:T(4,128)} %param.9) | copy-start | bytes 49156
Sparse Core Ops, SparseCore 0:
  9.9 39.2 all-gather.1
  247.5 43.5 reduce-scatter.1
where the time goes:
time: 303 us
  matrix products  97.5 us (32%)
  waiting for transfers between devices  85.6 us (28%)
  other arithmetic  74.2 us (24%)
  local copies, waits for them, and re-layouts  30 us (10%)
  between operations  14.1 us (5%)
    dot_general x16, matrix products, add_block(): jnp.dot(expand_bits(packed_cols), vector_rows, preferred_element_type=jnp...  97.5 us
    convert_element_type x16, other arithmetic, expand_bits(): bit_table.reshape(packed.shape[0], packed.shape[1] * 32)  70.8 us
    reduce_scatter x1, waiting for transfers between devices, shards(): lax.psum_scatter(partial_sum, 'row', scatter_dimension=0, tiled=True)  43.7 us
    all_gather x1, waiting for transfers between devices, shards(): lax.all_gather(frontier, 'col', axis=0, tiled=True)  41.2 us
    dynamic_slice x8, local copies, waits for them, and re-layouts, tile_product(): return lax.map(one_rows, row_blocks).reshape(row_total, vectors.shape[1])  20.1 us
  transfers between devices with their start and end apart: 2, of which 2 were waited for; matrix products, arithmetic and copies ran while one was open for 0% of the time, Pallas kernels for 0%

commit v1 on v0

--- a/solution.py
+++ b/solution.py
@@ -53,7 +53,12 @@
 
 
 def shards(adjacency, frontier, visited):
-    partial_sum = tile_product(adjacency, lax.all_gather(frontier, "col", axis=0, tiled=True))
+    partial_sum = tile_product(
+        adjacency,
+        jnp.concatenate(
+            lax.all_to_all(jnp.stack([frontier] * lax.axis_size("col")), "col", 0, 0), axis=0
+        ),
+    )
     reached = lax.psum_scatter(partial_sum, "row", scatter_dimension=0, tiled=True)
     return finish(reached, visited)
 

time: 303 us -> 319 us (1.053)
  waiting for transfers between devices: 85.6 us -> 93 us
  starting transfers between devices: 0.08 us -> 5.23 us
  local copies, waits for them, and re-layouts: 30 us -> 33.5 us
    all_to_all x0 -> x1, waiting for transfers between devices: none -> 49.1 us  [shards(): lax.all_to_all(jnp.stack([frontier] * lax.axis_size('col')), 'col', 0, 0)]
    all_gather x1 -> x0, waiting for transfers between devices: 41.2 us -> none  [shards(): lax.all_gather(frontier, 'col', axis=0, tiled=True)]
    all_to_all x0 -> x1, starting transfers between devices: none -> 5.2 us  [shards(): lax.all_to_all(jnp.stack([frontier] * lax.axis_size('col')), 'col', 0, 0)]
    another operation x0 -> x1, local copies, waits for them, and re-layouts: none -> 3.52 us  [shards(): jnp.stack([frontier] * lax.axis_size('col'))]
where the time goes in v1:
time: 319 us
  matrix products  97.5 us (31%)
  waiting for transfers between devices  93 us (29%)
  other arithmetic  74.4 us (23%)
  local copies, waits for them, and re-layouts  33.5 us (11%)
  between operations  14.1 us (4%)
  starting transfers between devices  5.23 us (2%)
    dot_general x16, matrix products, add_block(): jnp.dot(expand_bits(packed_cols), vector_rows, preferred_element_type=jnp...  97.5 us
    convert_element_type x16, other arithmetic, expand_bits(): bit_table.reshape(packed.shape[0], packed.shape[1] * 32)  71 us
    all_to_all x1, waiting for transfers between devices, shards(): lax.all_to_all(jnp.stack([frontier] * lax.axis_size('col')), 'col', 0, 0)  49.1 us
    reduce_scatter x1, waiting for transfers between devices, shards(): lax.psum_scatter(partial_sum, 'row', scatter_dimension=0, tiled=True)  43.9 us
    dynamic_slice x8, local copies, waits for them, and re-layouts, tile_product(): return lax.map(one_rows, row_blocks).reshape(row_total, vectors.shape[1])  20.1 us
  transfers between devices with their start and end apart: 2, of which 2 were waited for; matrix products, arithmetic and copies ran while one was open for 0% of the time, Pallas kernels for 0%

profile of v1, /device:TPU:0, one launch (start us, length us, event | category | flops | bytes accessed | tf_op | source)
XLA Modules:
  0.0 318.8 jit_solution(8991759900233269007)
XLA Ops:
  10.7 5.2 %all-to-all-start = ((bf16[8,2048,128]{2,1,0:T(8,128)(2,1)}), bf16[8,2048,128]{2,1,0:T(8,128)(2,1)}, u32[]{:S(2)}, u32[]{:S(2)}) async-start(bf16[8,2048,128]{2,1,0:T(8,128)(2,1)} %stack.2), calls=%async_computation | async-start | bytes 8388608 | tf_op jit(solution)/shard_map/all_to_all | solution.py:59
  15.9 49.1 %all-to-all-done = bf16[8,2048,128]{2,1,0:T(8,128)(2,1)} async-done(((bf16[8,2048,128]{2,1,0:T(8,128)(2,1)}), bf16[8,2048,128]{2,1,0:T(8,128)(2,1)}, u32[]{:S(2)}, u32[]{:S(2)}) %all-to-all-start) | async-done | bytes 4194336 | tf_op jit(solution)/shard_map/all_to_all | solution.py:59
  65.1 195.4 %while.36 = (s32[]{:T(128)}, f32[4,1024,128]{2,1,0:T(8,128)}, s32[4,1024,512]{2,1,0:T(8,128)}, bf16[16384,128]{1,0:T(8,128)(2,1)}, s32[]{:T(128)}, /*index=5*/s3...) while((s32[]{:T(128)}, f32[4,1024,128]{2,1,0:T(8,128)}, ...), condition=%wide.region_3.4_spmd, body=%wide.region_0.3_spmd.sunk | while | flops 1086586880 | bytes 29951060 | solution.py:36
  70.1 43.0 %while.37 = (s32[]{:T(128)}, f32[1024,128]{1,0:T(8,128)S(1)}, s32[1024,512]{0,1:T(8,128)S(1)}, bf16[16384,128]{1,0:T(8,128)(2,1)}, s32[]{:T(128)}, /*index=5*/s3...) while((s32[]{:T(128)}, f32[1024,128]{1,0:T(8,128)S(1)}, ...), condition=%wide.region_2.2_spmd.clone, body=%wide.region_1.1_spmd.clone.sunk | while | flops 1086586880 | bytes 20513124 | solution.py:34
  70.3 4.4 %fusion.66 = bf16[1024,4096]{0,1:T(8,128)(2,1)} fusion(s32[4096]{0:T(1024)S(1)} %shift_right_arithmetic.108, s32[1024,128]{0,1:T(8,128)S(1)} %constant_dynamic-slice_fusion.5), kind=kLoop, calls=%fused_computation.2.clone.1 | loop fusion | flops 12582912 | bytes 8929280 | tf_op jit(solution)/shard_map/while/body/eval_jaxpr/while/body/eval_jaxpr/convert_element_type | solution.py:12
  74.8 6.1 %convolution_add_fusion.2 = f32[1024,128]{1,0:T(8,128)S(1)} fusion(bf16[1024,4096]{0,1:T(8,128)(2,1)} %fusion.66, bf16[16384,128]{1,0:T(8,128)(2,1)} %get-tuple-element.340, s32[]{:T(128)S(6)} %select_n.46, f32[1024,128]{1,0:T(8,128)S(1)} %get-tuple-element.326, pred[]{:T(512)S(6)} %compare.13), kind=kOutput, calls=%fused_computation.3.clone.1 | convolution fusion | flops 1074003968 | bytes 10485765 | tf_op jit(solution)/shard_map/while/body/eval_jaxpr/while/body/eval_jaxpr/dot_general | solution.py:30
  81.1 4.4 %fusion.66 = bf16[1024,4096]{0,1:T(8,128)(2,1)} fusion(s32[4096]{0:T(1024)S(1)} %shift_right_arithmetic.108, s32[1024,128]{0,1:T(8,128)S(1)} %constant_dynamic-slice_fusion.5), kind=kLoop, calls=%fused_computation.2.clone.1 | loop fusion | flops 12582912 | bytes 8929280 | tf_op jit(solution)/shard_map/while/body/eval_jaxpr/while/body/eval_jaxpr/convert_element_type | solution.py:12
  85.5 6.1 %convolution_add_fusion.2 = f32[1024,128]{1,0:T(8,128)S(1)} fusion(bf16[1024,4096]{0,1:T(8,128)(2,1)} %fusion.66, bf16[16384,128]{1,0:T(8,128)(2,1)} %get-tuple-element.340, s32[]{:T(128)S(6)} %select_n.46, f32[1024,128]{1,0:T(8,128)S(1)} %get-tuple-element.326, pred[]{:T(512)S(6)} %compare.13), kind=kOutput, calls=%fused_computation.3.clone.1 | convolution fusion | flops 1074003968 | bytes 10485765 | tf_op jit(solution)/shard_map/while/body/eval_jaxpr/while/body/eval_jaxpr/dot_general | solution.py:30
  91.8 4.4 %fusion.66 = bf16[1024,4096]{0,1:T(8,128)(2,1)} fusion(s32[4096]{0:T(1024)S(1)} %shift_right_arithmetic.108, s32[1024,128]{0,1:T(8,128)S(1)} %constant_dynamic-slice_fusion.5), kind=kLoop, calls=%fused_computation.2.clone.1 | loop fusion | flops 12582912 | bytes 8929280 | tf_op jit(solution)/shard_map/while/body/eval_jaxpr/while/body/eval_jaxpr/convert_element_type | solution.py:12
  96.2 6.1 %convolution_add_fusion.2 = f32[1024,128]{1,0:T(8,128)S(1)} fusion(bf16[1024,4096]{0,1:T(8,128)(2,1)} %fusion.66, bf16[16384,128]{1,0:T(8,128)(2,1)} %get-tuple-element.340, s32[]{:T(128)S(6)} %select_n.46, f32[1024,128]{1,0:T(8,128)S(1)} %get-tuple-element.326, pred[]{:T(512)S(6)} %compare.13), kind=kOutput, calls=%fused_computation.3.clone.1 | convolution fusion | flops 1074003968 | bytes 10485765 | tf_op jit(solution)/shard_map/while/body/eval_jaxpr/while/body/eval_jaxpr/dot_general | solution.py:30
  102.5 4.4 %fusion.66 = bf16[1024,4096]{0,1:T(8,128)(2,1)} fusion(s32[4096]{0:T(1024)S(1)} %shift_right_arithmetic.108, s32[1024,128]{0,1:T(8,128)S(1)} %constant_dynamic-slice_fusion.5), kind=kLoop, calls=%fused_computation.2.clone.1 | loop fusion | flops 12582912 | bytes 8929280 | tf_op jit(solution)/shard_map/while/body/eval_jaxpr/while/body/eval_jaxpr/convert_element_type | solution.py:12
  107.0 6.1 %convolution_add_fusion.2 = f32[1024,128]{1,0:T(8,128)S(1)} fusion(bf16[1024,4096]{0,1:T(8,128)(2,1)} %fusion.66, bf16[16384,128]{1,0:T(8,128)(2,1)} %get-tuple-element.340, s32[]{:T(128)S(6)} %select_n.46, f32[1024,128]{1,0:T(8,128)S(1)} %get-tuple-element.326, pred[]{:T(512)S(6)} %compare.13), kind=kOutput, calls=%fused_computation.3.clone.1 | convolution fusion | flops 1074003968 | bytes 10485765 | tf_op jit(solution)/shard_map/while/body/eval_jaxpr/while/body/eval_jaxpr/dot_general | solution.py:30
  119.0 43.0 %while.37 = (s32[]{:T(128)}, f32[1024,128]{1,0:T(8,128)S(1)}, s32[1024,512]{0,1:T(8,128)S(1)}, bf16[16384,128]{1,0:T(8,128)(2,1)}, s32[]{:T(128)}, /*index=5*/s3...) while((s32[]{:T(128)}, f32[1024,128]{1,0:T(8,128)S(1)}, ...), condition=%wide.region_2.2_spmd.clone, body=%wide.region_1.1_spmd.clone.sunk | while | flops 1086586880 | bytes 20513124 | solution.py:34
  119.2 4.4 %fusion.66 = bf16[1024,4096]{0,1:T(8,128)(2,1)} fusion(s32[4096]{0:T(1024)S(1)} %shift_right_arithmetic.108, s32[1024,128]{0,1:T(8,128)S(1)} %constant_dynamic-slice_fusion.5), kind=kLoop, calls=%fused_computation.2.clone.1 | loop fusion | flops 12582912 | bytes 8929280 | tf_op jit(solution)/shard_map/while/body/eval_jaxpr/while/body/eval_jaxpr/convert_element_type | solution.py:12
  123.6 6.1 %convolution_add_fusion.2 = f32[1024,128]{1,0:T(8,128)S(1)} fusion(bf16[1024,4096]{0,1:T(8,128)(2,1)} %fusion.66, bf16[16384,128]{1,0:T(8,128)(2,1)} %get-tuple-element.340, s32[]{:T(128)S(6)} %select_n.46, f32[1024,128]{1,0:T(8,128)S(1)} %get-tuple-element.326, pred[]{:T(512)S(6)} %compare.13), kind=kOutput, calls=%fused_computation.3.clone.1 | convolution fusion | flops 1074003968 | bytes 10485765 | tf_op jit(solution)/shard_map/while/body/eval_jaxpr/while/body/eval_jaxpr/dot_general | solution.py:30
  129.9 4.4 %fusion.66 = bf16[1024,4096]{0,1:T(8,128)(2,1)} fusion(s32[4096]{0:T(1024)S(1)} %shift_right_arithmetic.108, s32[1024,128]{0,1:T(8,128)S(1)} %constant_dynamic-slice_fusion.5), kind=kLoop, calls=%fused_computation.2.clone.1 | loop fusion | flops 12582912 | bytes 8929280 | tf_op jit(solution)/shard_map/while/body/eval_jaxpr/while/body/eval_jaxpr/convert_element_type | solution.py:12
  134.4 6.1 %convolution_add_fusion.2 = f32[1024,128]{1,0:T(8,128)S(1)} fusion(bf16[1024,4096]{0,1:T(8,128)(2,1)} %fusion.66, bf16[16384,128]{1,0:T(8,128)(2,1)} %get-tuple-element.340, s32[]{:T(128)S(6)} %select_n.46, f32[1024,128]{1,0:T(8,128)S(1)} %get-tuple-element.326, pred[]{:T(512)S(6)} %compare.13), kind=kOutput, calls=%fused_computation.3.clone.1 | convolution fusion | flops 1074003968 | bytes 10485765 | tf_op jit(solution)/shard_map/while/body/eval_jaxpr/while/body/eval_jaxpr/dot_general | solution.py:30
  140.7 4.4 %fusion.66 = bf16[1024,4096]{0,1:T(8,128)(2,1)} fusion(s32[4096]{0:T(1024)S(1)} %shift_right_arithmetic.108, s32[1024,128]{0,1:T(8,128)S(1)} %constant_dynamic-slice_fusion.5), kind=kLoop, calls=%fused_computation.2.clone.1 | loop fusion | flops 12582912 | bytes 8929280 | tf_op jit(solution)/shard_map/while/body/eval_jaxpr/while/body/eval_jaxpr/convert_element_type | solution.py:12
  145.1 6.1 %convolution_add_fusion.2 = f32[1024,128]{1,0:T(8,128)S(1)} fusion(bf16[1024,4096]{0,1:T(8,128)(2,1)} %fusion.66, bf16[16384,128]{1,0:T(8,128)(2,1)} %get-tuple-element.340, s32[]{:T(128)S(6)} %select_n.46, f32[1024,128]{1,0:T(8,128)S(1)} %get-tuple-element.326, pred[]{:T(512)S(6)} %compare.13), kind=kOutput, calls=%fused_computation.3.clone.1 | convolution fusion | flops 1074003968 | bytes 10485765 | tf_op jit(solution)/shard_map/while/body/eval_jaxpr/while/body/eval_jaxpr/dot_general | solution.py:30
  151.4 4.4 %fusion.66 = bf16[1024,4096]{0,1:T(8,128)(2,1)} fusion(s32[4096]{0:T(1024)S(1)} %shift_right_arithmetic.108, s32[1024,128]{0,1:T(8,128)S(1)} %constant_dynamic-slice_fusion.5), kind=kLoop, calls=%fused_computation.2.clone.1 | loop fusion | flops 12582912 | bytes 8929280 | tf_op jit(solution)/shard_map/while/body/eval_jaxpr/while/body/eval_jaxpr/convert_element_type | solution.py:12
  155.8 6.1 %convolution_add_fusion.2 = f32[1024,128]{1,0:T(8,128)S(1)} fusion(bf16[1024,4096]{0,1:T(8,128)(2,1)} %fusion.66, bf16[16384,128]{1,0:T(8,128)(2,1)} %get-tuple-element.340, s32[]{:T(128)S(6)} %select_n.46, f32[1024,128]{1,0:T(8,128)S(1)} %get-tuple-element.326, pred[]{:T(512)S(6)} %compare.13), kind=kOutput, calls=%fused_computation.3.clone.1 | convolution fusion | flops 1074003968 | bytes 10485765 | tf_op jit(solution)/shard_map/while/body/eval_jaxpr/while/body/eval_jaxpr/dot_general | solution.py:30
  167.9 43.0 %while.37 = (s32[]{:T(128)}, f32[1024,128]{1,0:T(8,128)S(1)}, s32[1024,512]{0,1:T(8,128)S(1)}, bf16[16384,128]{1,0:T(8,128)(2,1)}, s32[]{:T(128)}, /*index=5*/s3...) while((s32[]{:T(128)}, f32[1024,128]{1,0:T(8,128)S(1)}, ...), condition=%wide.region_2.2_spmd.clone, body=%wide.region_1.1_spmd.clone.sunk | while | flops 1086586880 | bytes 20513124 | solution.py:34
  172.5 6.1 %convolution_add_fusion.2 = f32[1024,128]{1,0:T(8,128)S(1)} fusion(bf16[1024,4096]{0,1:T(8,128)(2,1)} %fusion.66, bf16[16384,128]{1,0:T(8,128)(2,1)} %get-tuple-element.340, s32[]{:T(128)S(6)} %select_n.46, f32[1024,128]{1,0:T(8,128)S(1)} %get-tuple-element.326, pred[]{:T(512)S(6)} %compare.13), kind=kOutput, calls=%fused_computation.3.clone.1 | convolution fusion | flops 1074003968 | bytes 10485765 | tf_op jit(solution)/shard_map/while/body/eval_jaxpr/while/body/eval_jaxpr/dot_general | solution.py:30
  183.2 6.1 %convolution_add_fusion.2 = f32[1024,128]{1,0:T(8,128)S(1)} fusion(bf16[1024,4096]{0,1:T(8,128)(2,1)} %fusion.66, bf16[16384,128]{1,0:T(8,128)(2,1)} %get-tuple-element.340, s32[]{:T(128)S(6)} %select_n.46, f32[1024,128]{1,0:T(8,128)S(1)} %get-tuple-element.326, pred[]{:T(512)S(6)} %compare.13), kind=kOutput, calls=%fused_computation.3.clone.1 | convolution fusion | flops 1074003968 | bytes 10485765 | tf_op jit(solution)/shard_map/while/body/eval_jaxpr/while/body/eval_jaxpr/dot_general | solution.py:30
  194.0 6.1 %convolution_add_fusion.2 = f32[1024,128]{1,0:T(8,128)S(1)} fusion(bf16[1024,4096]{0,1:T(8,128)(2,1)} %fusion.66, bf16[16384,128]{1,0:T(8,128)(2,1)} %get-tuple-element.340, s32[]{:T(128)S(6)} %select_n.46, f32[1024,128]{1,0:T(8,128)S(1)} %get-tuple-element.326, pred[]{:T(512)S(6)} %compare.13), kind=kOutput, calls=%fused_computation.3.clone.1 | convolution fusion | flops 1074003968 | bytes 10485765 | tf_op jit(solution)/shard_map/while/body/eval_jaxpr/while/body/eval_jaxpr/dot_general | solution.py:30
  204.7 6.1 %convolution_add_fusion.2 = f32[1024,128]{1,0:T(8,128)S(1)} fusion(bf16[1024,4096]{0,1:T(8,128)(2,1)} %fusion.66, bf16[16384,128]{1,0:T(8,128)(2,1)} %get-tuple-element.340, s32[]{:T(128)S(6)} %select_n.46, f32[1024,128]{1,0:T(8,128)S(1)} %get-tuple-element.326, pred[]{:T(512)S(6)} %compare.13), kind=kOutput, calls=%fused_computation.3.clone.1 | convolution fusion | flops 1074003968 | bytes 10485765 | tf_op jit(solution)/shard_map/while/body/eval_jaxpr/while/body/eval_jaxpr/dot_general | solution.py:30
  216.7 43.0 %while.37 = (s32[]{:T(128)}, f32[1024,128]{1,0:T(8,128)S(1)}, s32[1024,512]{0,1:T(8,128)S(1)}, bf16[16384,128]{1,0:T(8,128)(2,1)}, s32[]{:T(128)}, /*index=5*/s3...) while((s32[]{:T(128)}, f32[1024,128]{1,0:T(8,128)S(1)}, ...), condition=%wide.region_2.2_spmd.clone, body=%wide.region_1.1_spmd.clone.sunk | while | flops 1086586880 | bytes 20513124 | solution.py:34
  221.3 6.1 %convolution_add_fusion.2 = f32[1024,128]{1,0:T(8,128)S(1)} fusion(bf16[1024,4096]{0,1:T(8,128)(2,1)} %fusion.66, bf16[16384,128]{1,0:T(8,128)(2,1)} %get-tuple-element.340, s32[]{:T(128)S(6)} %select_n.46, f32[1024,128]{1,0:T(8,128)S(1)} %get-tuple-element.326, pred[]{:T(512)S(6)} %compare.13), kind=kOutput, calls=%fused_computation.3.clone.1 | convolution fusion | flops 1074003968 | bytes 10485765 | tf_op jit(solution)/shard_map/while/body/eval_jaxpr/while/body/eval_jaxpr/dot_general | solution.py:30
  232.1 6.1 %convolution_add_fusion.2 = f32[1024,128]{1,0:T(8,128)S(1)} fusion(bf16[1024,4096]{0,1:T(8,128)(2,1)} %fusion.66, bf16[16384,128]{1,0:T(8,128)(2,1)} %get-tuple-element.340, s32[]{:T(128)S(6)} %select_n.46, f32[1024,128]{1,0:T(8,128)S(1)} %get-tuple-element.326, pred[]{:T(512)S(6)} %compare.13), kind=kOutput, calls=%fused_computation.3.clone.1 | convolution fusion | flops 1074003968 | bytes 10485765 | tf_op jit(solution)/shard_map/while/body/eval_jaxpr/while/body/eval_jaxpr/dot_general | solution.py:30
  242.8 6.1 %convolution_add_fusion.2 = f32[1024,128]{1,0:T(8,128)S(1)} fusion(bf16[1024,4096]{0,1:T(8,128)(2,1)} %fusion.66, bf16[16384,128]{1,0:T(8,128)(2,1)} %get-tuple-element.340, s32[]{:T(128)S(6)} %select_n.46, f32[1024,128]{1,0:T(8,128)S(1)} %get-tuple-element.326, pred[]{:T(512)S(6)} %compare.13), kind=kOutput, calls=%fused_computation.3.clone.1 | convolution fusion | flops 1074003968 | bytes 10485765 | tf_op jit(solution)/shard_map/while/body/eval_jaxpr/while/body/eval_jaxpr/dot_general | solution.py:30
  253.6 6.1 %convolution_add_fusion.2 = f32[1024,128]{1,0:T(8,128)S(1)} fusion(bf16[1024,4096]{0,1:T(8,128)(2,1)} %fusion.66, bf16[16384,128]{1,0:T(8,128)(2,1)} %get-tuple-element.340, s32[]{:T(128)S(6)} %select_n.46, f32[1024,128]{1,0:T(8,128)S(1)} %get-tuple-element.326, pred[]{:T(512)S(6)} %compare.13), kind=kOutput, calls=%fused_computation.3.clone.1 | convolution fusion | flops 1074003968 | bytes 10485765 | tf_op jit(solution)/shard_map/while/body/eval_jaxpr/while/body/eval_jaxpr/dot_general | solution.py:30
  263.5 43.9 %reduce-scatter.2.cloned.1.call-done = f32[1024,128]{0,1:T(8,128)} async-done(((f32[4096,128]{0,1:T(8,128)}), f32[1024,128]{0,1:T(8,128)}) %reduce-scatter.2.cloned.1.call-update) | async-done | bytes 524304 | tf_op jit(solution)/shard_map/reduce_scatter | solution.py:62
  (87 shorter events, 72.4 us)
Async XLA Ops:
  10.7 54.4 %all-to-all-start = ((bf16[8,2048,128]{2,1,0:T(8,128)(2,1)}), bf16[8,2048,128]{2,1,0:T(8,128)(2,1)}, u32[]{:S(2)}, u32[]{:S(2)}) async-start(bf16[8,2048,128]{2,1,0:T(8,128)(2,1)} %stack.2), calls=%async_computation | async-start | bytes 8388608 | tf_op jit(solution)/shard_map/all_to_all | solution.py:59
  15.9 291.5 %reduce-scatter.2.cloned.1.call-start = ((), (), s32[]{:S(2)}) async-start(), calls=%async_computation.2 | async-start | bytes 2621440 | tf_op jit(solution)/shard_map/reduce_scatter | solution.py:62
  260.5 46.9 %copy-start = (s32[4,1024]{1,0:T(4,128)S(1)}, s32[4,1024]{1,0:T(4,128)}, u32[]{:S(2)}) copy-start(s32[4,1024]{1,0:T(4,128)} %param.9) | copy-start | bytes 49156
Sparse Core Ops, SparseCore 0:
  263.6 43.7 reduce-scatter.1
